TPU v7x, 32 devices: a whole 2x2x4 slice. The times are simulated.
32 devices in a mesh: wide: 8 (over z, core), narrow: 4 (over y, x).
Axes of the slice: x: 2, y: 2, z: 4, core: 2. Of those that a mesh axis runs over, the one named last changes fastest.
Arguments:
- tridiag_vectors: float32 [128, 131072], P(('wide', 'narrow')), may hold values from -6 to 6
- reflectors: float32 [2, 131072, 256], P(None, 'wide'), may hold values from -0.015625 to 0.015625
- triangles: float32 [2, 256, 256], replicated, as said below
- lower_blocks: float32 [6, 1536, 1536], P(None, 'wide'), may hold values from -0.109375 to 0.109375
- diag_inverses: float32 [4, 1536, 1536], P(None, None, 'wide'), as said below
Outputs:
- transformed: float32 [128, 131072], P('narrow', 'wide')
- solved: float32 [128, 4, 1536], P('narrow', None, 'wide')
Inputs may be any that keep to these rules, and one draw needn't show every extreme that they name: `triangles`: zero below the diagonal, positive on it. `diag_inverses`: zero above the diagonal, positive on it.
All inputs are finite; a program needn't handle non-finite values.
Results may differ from a plain program's by a relative error of at most 0.00019.
Values sent between devices are 32-bit elements; how exact they have to be, the bound alone decides.
A program may use at most 128 MiB of HBM per device.

v0:
```python
import jax
import jax.numpy as jnp
from jax import lax
from jax.sharding import PartitionSpec as P

HIGHEST = lax.Precision.HIGHEST


def reflect(current, vectors, factor, products):
    coeffs = jnp.dot(products, factor.T, precision=HIGHEST)
    return current - jnp.dot(coeffs, vectors.T, precision=HIGHEST)


def add_piece(inverse, segment):
    return jnp.dot(segment, inverse, precision=HIGHEST)


def solve_chain(corner, lower_blocks, diag_inverses):
    local_count, panels, share_cols = corner.shape
    zeroed = jnp.zeros((local_count, share_cols), jnp.float32)
    pending = [zeroed] * panels
    results = [zeroed] * panels
    for source in reversed(range(panels)):
        remain = corner[:, source, :] - pending[source]
        solution = add_piece(
            diag_inverses[source], lax.all_gather(remain, "wide", axis=1, tiled=True)
        )
        results[source] = solution
        if source > 0:
            offset = source * (source - 1) // 2
            blocks = lower_blocks[offset : offset + source]
            partial_terms = jnp.einsum("ks,qsc->kqc", solution, blocks, precision=HIGHEST)
            scattered = lax.psum_scatter(partial_terms, "wide", scatter_dimension=2, tiled=True)
            for target in range(source):
                pending[target] = pending[target] + scattered[:, target, :]
    return jnp.stack(results, axis=1)


def body(tridiag_vectors, reflectors, triangles, lower_blocks, diag_inverses):
    wide_size = lax.axis_size("wide")
    spread = lax.all_to_all(
        tridiag_vectors, ("wide", "narrow"), split_axis=1, concat_axis=0, tiled=True
    )
    current = lax.all_to_all(spread, "narrow", split_axis=0, concat_axis=1, tiled=True)
    for which in (1, 0):
        products = lax.psum(jnp.dot(current, reflectors[which], precision=HIGHEST), "wide")
        current = reflect(current, reflectors[which], triangles[which], products)
    panels, panel_rows, share_cols = diag_inverses.shape
    corner_span = panels * panel_rows
    tail_cols = current[:, current.shape[1] - corner_span :]
    framed = tail_cols.reshape(tail_cols.shape[0], panels, wide_size, share_cols)
    received = lax.all_to_all(framed, "wide", split_axis=2, concat_axis=2, tiled=True)
    corner = received[:, :, wide_size - 1, :]
    solved = solve_chain(corner, lower_blocks, diag_inverses)
    return (current, solved)


def solution(mesh):
    placed = (
        P(("wide", "narrow"), None),
        P(None, "wide", None),
        P(),
        P(None, "wide", None),
        P(None, None, "wide"),
    )
    return jax.shard_map(
        body,
        mesh=mesh,
        in_specs=placed,
        out_specs=(P("narrow", "wide"), P("narrow", None, "wide")),
        check_vma=False,
    )
```

profile of v0, /device:TPU:0, one launch (start us, length us, event | category | flops | bytes accessed | tf_op | source)
XLA Modules:
  0.0 433.0 jit_solution(8765695923981802089)
XLA Ops:
  7.2 56.5 %all_to_all.40 = f32[4,32,4096]{2,0,1:T(4,128)} all-to-all(f32[4,32,4096]{2,0,1:T(4,128)} %bitcast.93), channel_id=1, replica_groups=mesh['wide'=8,'narrow'=4] {'wide','narrow'}, dimensions={1} | all-to-all | bytes 4194304 | tf_op jit(solution)/shard_map/all_to_all | solution.py:41
  65.6 28.2 %all_to_all.41 = f32[4,32,4096]{2,1,0:T(8,128)S(1)} all-to-all(f32[4,32,4096]{2,1,0:T(8,128)S(1)} %all_to_all.32), channel_id=1, replica_groups=mesh['wide'=8,'narrow'=4] {'narrow'}, dimensions={0} | all-to-all | bytes 4194304 | tf_op jit(solution)/shard_map/all_to_all | solution.py:44
  95.3 10.7 %fusion.4 = f32[32,256]{1,0:T(8,128)S(1)} fusion(f32[32,16384]{1,0:T(8,128)S(1)} %bitcast.83, f32[2,16384,256]{2,1,0:T(8,128)} %param.6), kind=kOutput, calls=%fused_computation.6 | convolution fusion | flops 1610612736 | bytes 18907136 | tf_op jit(solution)/shard_map/dot_general | solution.py:46
  106.0 26.1 %psum.14 = f32[32,256]{1,0:T(8,128)S(1)} all-reduce(f32[32,256]{1,0:T(8,128)S(1)} %fusion.4), channel_id=1, replica_groups=mesh['wide'=8,'narrow'=4] {'wide'}, use_global_device_ids=true, to_apply=%region_0.0 | all-reduce | flops 8192 | bytes 65536 | tf_op jit(solution)/shard_map/psum | solution.py:46
  132.5 18.6 %convolution_subtract_fusion.1 = f32[32,16384]{1,0:T(8,128)S(1)} fusion(f32[32,16384]{1,0:T(8,128)} %bitcast.84, f32[32,256]{1,0:T(8,128)S(1)} %fusion.33, f32[2,16384,256]{2,1,0:T(8,128)} %param.6), kind=kOutput, calls=%fused_computation.1 | convolution fusion | flops 1611137024 | bytes 21004288 | tf_op jit(solution)/shard_map/dot_general | solution.py:11
  151.1 10.6 %fusion.1 = f32[32,256]{1,0:T(8,128)S(1)} fusion(f32[32,16384]{1,0:T(8,128)S(1)} %convolution_subtract_fusion.1, f32[2,16384,256]{2,1,0:T(8,128)} %param.6), kind=kOutput, calls=%fused_computation.3 | convolution fusion | flops 1610612736 | bytes 18907136 | tf_op jit(solution)/shard_map/dot_general | solution.py:46
  161.8 26.2 %psum.15 = f32[32,256]{1,0:T(8,128)S(1)} all-reduce(f32[32,256]{1,0:T(8,128)S(1)} %fusion.1), channel_id=1, replica_groups=mesh['wide'=8,'narrow'=4] {'wide'}, use_global_device_ids=true, to_apply=%region_1.0 | all-reduce | flops 8192 | bytes 65536 | tf_op jit(solution)/shard_map/psum | solution.py:46
  188.3 17.3 %convolution_subtract_fusion = f32[32,16384]{1,0:T(8,128)S(1)} fusion(f32[32,16384]{1,0:T(8,128)S(1)} %convolution_subtract_fusion.1, f32[32,256]{1,0:T(8,128)S(1)} %fusion.31, f32[2,16384,256]{2,1,0:T(8,128)} %param.6), kind=kOutput, calls=%fused_computation | convolution fusion | flops 1611137024 | bytes 21004288 | tf_op jit(solution)/shard_map/dot_general | solution.py:11
  208.0 29.0 %all_to_all.42 = f32[32,4,8,192]{3,0,1,2:T(8,128)S(1)} all-to-all(f32[32,4,8,192]{3,0,1,2:T(8,128)S(1)} %copy.22), channel_id=1, replica_groups=mesh['wide'=8,'narrow'=4] {'wide'}, dimensions={2} | all-to-all | bytes 1572864 | tf_op jit(solution)/shard_map/all_to_all | solution.py:52
  237.1 15.7 %all-gather = f32[32,1,1536]{0,1,2:T(1,128)S(1)} all-gather(f32[32,1,192]{0,1,2:T(1,128)S(1)} %copy.23), channel_id=2, replica_groups=mesh['wide'=8,'narrow'=4] {'wide'}, dimensions={2}, use_global_device_ids=true | all-gather | bytes 221184 | tf_op jit(solution)/shard_map/all_gather | solution.py:26
  252.9 2.6 fusion.21
  255.5 5.0 %fusion.10 = f32[32,3,1536]{2,0,1:T(8,128)} fusion(f32[6,192,1536]{2,1,0:T(8,128)} %param.8, f32[32,192]{1,0:T(8,128)S(1)} %fusion.21), kind=kOutput, calls=%fused_computation.12 | convolution fusion | flops 339738624 | bytes 4153344 | tf_op jit(solution)/shard_map/ks,qsc->kqc/dot_general | solution.py:32
  260.5 2.6 copy.28
  265.5 29.5 %reduce-scatter.10.cloned.1.call-done = f32[192,96]{1,0:T(8,128)} async-done(((f32[1536,96]{1,0:T(8,128)}), f32[192,96]{1,0:T(8,128)}) %reduce-scatter.10.cloned.1.call-update) | async-done | bytes 73744
  296.5 16.0 %all-gather.1 = f32[32,1,1536]{0,1,2:T(1,128)S(1)} all-gather(f32[32,1,192]{0,1,2:T(1,128)S(1)} %copy.24), channel_id=3, replica_groups=mesh['wide'=8,'narrow'=4] {'wide'}, dimensions={2}, use_global_device_ids=true | all-gather | bytes 221184 | tf_op jit(solution)/shard_map/all_gather | solution.py:26
  312.5 2.6 fusion.19
  315.1 3.2 fusion.12
  321.0 30.2 %reduce-scatter.12.cloned.1.call-done = f32[192,64]{1,0:T(8,128)} async-done(((f32[1536,64]{1,0:T(8,128)}), f32[192,64]{1,0:T(8,128)}) %reduce-scatter.12.cloned.1.call-update) | async-done | bytes 49168
  352.6 15.7 %all-gather.2 = f32[32,1,1536]{0,1,2:T(1,128)S(1)} all-gather(f32[32,1,192]{0,1,2:T(1,128)S(1)} %copy.25), channel_id=4, replica_groups=mesh['wide'=8,'narrow'=4] {'wide'}, dimensions={2}, use_global_device_ids=true | all-gather | bytes 221184 | tf_op jit(solution)/shard_map/all_gather | solution.py:26
  368.4 2.6 fusion.17
  371.0 4.8 %convolution_bitcast_fusion = f32[1536,32]{1,0:T(8,128)} fusion(f32[32,192]{1,0:T(8,128)S(1)} %fusion.17, f32[6,192,1536]{2,1,0:T(8,128)} %param.8), kind=kOutput, calls=%fused_computation.14 | convolution fusion | flops 113246208 | bytes 1400832 | tf_op jit(solution)/shard_map/ks,qsc->kqc/dot_general | solution.py:32
  375.9 30.3 %reduce-scatter.14.cloned.1.call-done = f32[192,32]{1,0:T(8,128)} async-done(((f32[1536,32]{1,0:T(8,128)}), f32[192,32]{1,0:T(8,128)}) %reduce-scatter.14.cloned.1.call-update) | async-done | bytes 24592
  407.3 15.7 %all-gather.3 = f32[32,1,1536]{0,1,2:T(1,128)S(1)} all-gather(f32[32,1,192]{0,1,2:T(1,128)S(1)} %copy.26), channel_id=5, replica_groups=mesh['wide'=8,'narrow'=4] {'wide'}, dimensions={2}, use_global_device_ids=true | all-gather | bytes 221184 | tf_op jit(solution)/shard_map/all_gather | solution.py:26
  423.1 2.6 fusion.28
  (43 shorter events, 16.5 us)
Async XLA Ops:
  7.2 287.9 %reduce-scatter.10.cloned.1.call-start = ((), (), s32[]{:S(2)}) async-start(), calls=%async_computation.6 | async-start | bytes 884736
  94.0 1.3 copy-start
  95.3 36.8 %copy-start.2 = (f32[2,256,256]{2,1,0:T(8,128)S(1)}, f32[2,256,256]{2,1,0:T(8,128)}, u32[]{:S(2)}) copy-start(f32[2,256,256]{2,1,0:T(8,128)} %param.7) | copy-start | bytes 1572868
  205.5 1.3 copy-start.1
  265.4 85.8 %reduce-scatter.12.cloned.1.call-start = ((), (), s32[]{:S(2)}) async-start(), calls=%async_computation.7 | async-start | bytes 884736
  320.9 85.4 %reduce-scatter.14.cloned.1.call-start = ((), (), s32[]{:S(2)}) async-start(), calls=%async_computation.8 | async-start | bytes 884736
Sparse Core Ops, SparseCore 0:
  265.6 29.4 reduce-scatter.9
  321.0 30.1 reduce-scatter.11
  375.9 30.2 reduce-scatter.13
where the time goes:
time: 434 us; the launch traced here: 433 us
  blocking collectives  229 us (53%)
  waiting for transfers between devices  90.1 us (21%)
  matrix products  81.5 us (19%)
  local copies, waits for them, and re-layouts  18.2 us (4%)
  between operations  14 us (3%)
    unnamed x6, waiting for transfers between devices  90.1 us
    all_gather x4, blocking collectives, solve_chain(): lax.all_gather(remain, 'wide', axis=1, tiled=True)  63.2 us
    all_to_all x1, blocking collectives, body(): lax.all_to_all(tridiag_vectors, ('wide', 'narrow'), split_axis=1, concat_...  56.5 us
    psum x2, blocking collectives, body(): lax.psum(jnp.dot(current, reflectors[which], precision=HIGHEST), 'wide')  52.3 us
    dot_general x2, matrix products, reflect(): return current - jnp.dot(coeffs, vectors.T, precision=HIGHEST)  35.9 us
    all_to_all x1, blocking collectives, body(): lax.all_to_all(framed, 'wide', split_axis=2, concat_axis=2, tiled=True)  29 us
    all_to_all x1, blocking collectives, body(): lax.all_to_all(spread, 'narrow', split_axis=0, concat_axis=1, tiled=True)  28.2 us
    dot_general x2, matrix products, body(): jnp.dot(current, reflectors[which], precision=HIGHEST)  21.3 us
  transfers between devices with their start and end apart: 3, of which 3 were waited for; matrix products, arithmetic and copies ran while one was open for 0% of the time, Pallas kernels for 0%

commit v1 on v0

v1 whole, which is shorter than its diff:
```python
import functools

import jax
import jax.numpy as jnp
from jax import lax
from jax.experimental import pallas as pl
from jax.experimental.pallas import tpu as pltpu
from jax.sharding import PartitionSpec as P

HIGHEST = lax.Precision.HIGHEST
MESH = pl.DeviceIdType.MESH
ANY = pl.ANY
VMEM = pltpu.VMEM


def greet(axes):
    barrier = pltpu.get_barrier_semaphore()
    total = 0
    for axis, size in axes:
        here = lax.axis_index(axis)
        for k in range(1, size):
            pl.semaphore_signal(
                barrier, inc=1, device_id={axis: lax.rem(here + k, size)}, device_id_type=MESH
            )
        total += size - 1
    pl.semaphore_wait(barrier, total)


def remote(src, dst, send, recv, axis, target):
    return pltpu.make_async_remote_copy(
        src_ref=src, dst_ref=dst, send_sem=send, recv_sem=recv,
        device_id={axis: target}, device_id_type=MESH,
    )


def spread_kernel(wide, narrow, z_ref, buf_ref, bounce, send1, recv1, send2, recv2, local_sem):
    w = lax.axis_index("wide")
    n = lax.axis_index("narrow")
    cols = buf_ref.shape[2]

    def piece(target):
        return z_ref.at[:, pl.ds(pl.multiple_of(target * cols, 128), cols)]

    def owner(source):
        return (source * narrow + n) // wide

    def slot(source):
        return (source * narrow + n) % wide

    greet((("wide", wide), ("narrow", narrow)))
    place = jnp.where(owner(w) == n, slot(w), wide + w)
    for k in range(1, wide):
        target = lax.rem(w + k, wide)
        remote(piece(target), buf_ref.at[place], send1.at[k], recv1.at[w], "wide", target).start()

    mine = owner(w) == n

    @pl.when(mine)
    def _():
        first = pltpu.make_async_copy(piece(w), bounce, local_sem.at[0])
        first.start()
        first.wait()
        pltpu.make_async_copy(bounce, buf_ref.at[slot(w)], local_sem.at[1]).start()

    @pl.when(jnp.logical_not(mine))
    def _():
        s = slot(w)
        remote(piece(w), buf_ref.at[s], send2.at[w], recv2.at[s], "narrow", owner(w)).start()

    for k in range(1, wide):
        source = lax.rem(w + k, wide)
        to = owner(source)
        s = slot(source)
        here = jnp.where(to == n, s, wide + source)
        remote(piece(source), buf_ref.at[here], send1.at[k], recv1.at[source], "wide", source).wait_recv()

        @pl.when(to != n)
        def _():
            remote(
                buf_ref.at[wide + source], buf_ref.at[s], send2.at[source], recv2.at[s], "narrow", to
            ).start()

    for k in range(1, wide):
        target = lax.rem(w + k, wide)
        remote(piece(target), buf_ref.at[place], send1.at[k], recv1.at[w], "wide", target).wait_send()
    for source in range(wide):
        to = owner(source)

        @pl.when(to != n)
        def _():
            remote(
                buf_ref.at[wide + source], buf_ref.at[source], send2.at[source], recv2.at[source],
                "narrow", to,
            ).wait_send()

    for s in range(wide):
        came = (n * wide + s) % narrow

        @pl.when(came != n)
        def _():
            remote(
                buf_ref.at[s], buf_ref.at[s], send2.at[s], recv2.at[s], "narrow", came
            ).wait_recv()

    @pl.when(mine)
    def _():
        pltpu.make_async_copy(bounce, buf_ref.at[slot(w)], local_sem.at[1]).wait()


def spread(z, wide, narrow):
    rows, order = z.shape
    cols = order // wide
    buf = pl.pallas_call(
        functools.partial(spread_kernel, wide, narrow),
        out_shape=jax.ShapeDtypeStruct((2 * wide, rows, cols), jnp.float32),
        in_specs=[pl.BlockSpec(memory_space=ANY)],
        out_specs=pl.BlockSpec(memory_space=ANY),
        scratch_shapes=[
            VMEM((rows, cols), jnp.float32),
            pltpu.SemaphoreType.DMA((wide,)),
            pltpu.SemaphoreType.DMA((wide,)),
            pltpu.SemaphoreType.DMA((wide,)),
            pltpu.SemaphoreType.DMA((wide,)),
            pltpu.SemaphoreType.DMA((2,)),
        ],
        compiler_params=pltpu.CompilerParams(collective_id=0, has_side_effects=True),
    )(z)
    return buf[:wide].reshape(wide * rows, cols)


def coeffs_kernel(wide, x_ref, t_ref, out_ref, slots, send, recv):
    w = lax.axis_index("wide")
    greet((("wide", wide),))
    for k in range(1, wide):
        target = lax.rem(w + k, wide)
        remote(x_ref, slots.at[w], send.at[k], recv.at[w], "wide", target).start()
    total = x_ref[...]
    for k in range(1, wide):
        source = lax.rem(w + k, wide)
        remote(x_ref, slots.at[source], send.at[k], recv.at[source], "wide", source).wait_recv()
        total = total + slots[source]
    out_ref[...] = lax.dot_general(
        total, t_ref[...], (((1,), (1,)), ((), ())),
        precision=HIGHEST, preferred_element_type=jnp.float32,
    )
    for k in range(1, wide):
        target = lax.rem(w + k, wide)
        remote(x_ref, slots.at[w], send.at[k], recv.at[w], "wide", target).wait_send()


def coeffs_of(products, factor, wide, which):
    return pl.pallas_call(
        functools.partial(coeffs_kernel, wide),
        out_shape=jax.ShapeDtypeStruct(products.shape, jnp.float32),
        in_specs=[pl.BlockSpec(memory_space=VMEM)] * 2,
        out_specs=pl.BlockSpec(memory_space=VMEM),
        scratch_shapes=[
            VMEM((wide,) + products.shape, jnp.float32),
            pltpu.SemaphoreType.DMA((wide,)),
            pltpu.SemaphoreType.DMA((wide,)),
        ],
        compiler_params=pltpu.CompilerParams(collective_id=1 + which, has_side_effects=True),
    )(products, factor)


def chain_kernel(
    wide, corner, lower, diag, out_ref, low_v, diag_v, own, gath, part, land,
    c_send, c_recv, g_send, g_recv, r_send, r_recv, low_sem, diag_sem,
):
    w = lax.axis_index("wide")
    panels, _, count, share = corner.shape
    last = wide - 1
    blocks = lower.shape[0]
    greet((("wide", wide),))

    @pl.when(w == last)
    def _():
        for p in reversed(range(panels)):
            for t in range(last):
                remote(
                    corner.at[p, t], own.at[p], c_send.at[p * wide + t], c_recv.at[p], "wide", t
                ).start()

    def diag_copy(p):
        return pltpu.make_async_copy(diag.at[p], diag_v.at[p], diag_sem.at[p])

    def low_copy(i):
        return pltpu.make_async_copy(lower.at[i], low_v.at[i], low_sem.at[i])

    for p in reversed(range(panels)):
        diag_copy(p).start()
        for q in range(p):
            low_copy(p * (p - 1) // 2 + q).start()

    def gather_copy(p, at, k, target):
        return remote(
            gath.at[p, at], gath.at[p, at], g_send.at[p * wide + k], g_recv.at[p * wide + at],
            "wide", target,
        )

    def reduce_copy(q, at, slot, k, target):
        return remote(
            part.at[q, at], land.at[q, slot], r_send.at[q * wide + k], r_recv.at[q * wide + slot],
            "wide", target,
        )

    def dot(a, b):
        return jnp.dot(a, b, precision=HIGHEST, preferred_element_type=jnp.float32)

    results = [None] * panels
    for p in reversed(range(panels)):

        @pl.when(w == last)
        def _():
            own[p] = corner[p, last]

        @pl.when(w != last)
        def _():
            remote(
                corner.at[p, 0], own.at[p], c_send.at[p * wide], c_recv.at[p], "wide", last
            ).wait_recv()

        remain = own[p]
        if p < panels - 1:
            summed = part[p, w]
            for k in range(1, wide):
                source = lax.rem(w + k, wide)
                reduce_copy(p, source, source, k, source).wait_recv()
                summed = summed + land[p, source]
            remain = remain - summed
        gath[p, w] = remain
        for k in range(1, wide):
            gather_copy(p, w, k, lax.rem(w + k, wide)).start()
        diag_copy(p).wait()

        def rows(source):
            return diag_v[p, pl.ds(pl.multiple_of(source * share, 8), share), :]

        def step(k, acc):
            source = lax.rem(w + k, wide)
            gather_copy(p, source, k, source).wait_recv()
            return acc + dot(gath[p, source], rows(source))

        solved = lax.fori_loop(1, wide, step, dot(remain, rows(w)))
        results[p] = solved
        out_ref[p] = solved
        if p > 0:
            target = p - 1
            total = None
            for j in range(panels - 1, target, -1):
                i = j * (j - 1) // 2 + target
                low_copy(i).wait()
                term = dot(results[j], low_v[i])
                total = term if total is None else total + term
            for t in range(wide):
                part[target, t] = total[:, t * share : (t + 1) * share]
            for k in range(1, wide):
                t = lax.rem(w + k, wide)
                reduce_copy(target, t, w, k, t).start()

    for p in range(panels):
        for k in range(1, wide):
            t = lax.rem(w + k, wide)
            gather_copy(p, w, k, t).wait_send()
            if p < panels - 1:
                reduce_copy(p, t, w, k, t).wait_send()

    @pl.when(w == last)
    def _():
        for p in range(panels):
            for t in range(last):
                remote(
                    corner.at[p, t], own.at[p], c_send.at[p * wide + t], c_recv.at[p], "wide", t
                ).wait_send()


def chain(corner, lower_blocks, diag_inverses, wide):
    panels, _, count, share = corner.shape
    dma = pltpu.SemaphoreType.DMA
    tile = (count, share)
    return pl.pallas_call(
        functools.partial(chain_kernel, wide),
        out_shape=jax.ShapeDtypeStruct((panels,) + tile, jnp.float32),
        in_specs=[
            pl.BlockSpec(memory_space=VMEM),
            pl.BlockSpec(memory_space=ANY),
            pl.BlockSpec(memory_space=ANY),
        ],
        out_specs=pl.BlockSpec(memory_space=VMEM),
        scratch_shapes=[
            VMEM(lower_blocks.shape, jnp.float32),
            VMEM(diag_inverses.shape, jnp.float32),
            VMEM((panels,) + tile, jnp.float32),
            VMEM((panels, wide) + tile, jnp.float32),
            VMEM((panels - 1, wide) + tile, jnp.float32),
            VMEM((panels - 1, wide) + tile, jnp.float32),
            dma((panels * wide,)),
            dma((panels,)),
            dma((panels * wide,)),
            dma((panels * wide,)),
            dma(((panels - 1) * wide,)),
            dma(((panels - 1) * wide,)),
            dma((lower_blocks.shape[0],)),
            dma((panels,)),
        ],
        compiler_params=pltpu.CompilerParams(
            collective_id=3, has_side_effects=True, vmem_limit_bytes=48 * 1024 * 1024
        ),
    )(corner, lower_blocks, diag_inverses)


def body(tridiag_vectors, reflectors, triangles, lower_blocks, diag_inverses):
    wide = lax.axis_size("wide")
    narrow = lax.axis_size("narrow")
    current = spread(tridiag_vectors, wide, narrow)
    for which in (1, 0):
        products = jnp.dot(current, reflectors[which], precision=HIGHEST)
        coeffs = coeffs_of(products, triangles[which], wide, which)
        current = current - jnp.dot(coeffs, reflectors[which].T, precision=HIGHEST)
    panels, panel_rows, share = diag_inverses.shape
    tail = current[:, current.shape[1] - panels * panel_rows :]
    corner = tail.reshape(tail.shape[0], panels, wide, share).transpose(1, 2, 0, 3)
    solved = chain(corner, lower_blocks, diag_inverses, wide)
    return current, solved.transpose(1, 0, 2)


def solution(mesh):
    placed = (
        P(("wide", "narrow"), None),
        P(None, "wide", None),
        P(),
        P(None, "wide", None),
        P(None, None, "wide"),
    )
    return jax.shard_map(
        body,
        mesh=mesh,
        in_specs=placed,
        out_specs=(P("narrow", "wide"), P("narrow", None, "wide")),
        check_vma=False,
    )
```

time: 434 us -> 238 us (0.55)
  blocking collectives: 229 us -> 0 us
  Pallas kernels: 0 us -> 159 us
  waiting for transfers between devices: 90.1 us -> 0 us
  matrix products: 81.5 us -> 59.3 us
  between operations: 14 us -> 0.72 us
    pallas_call x0 -> x4, Pallas kernels: none -> 159 us  [the longest x1 67.5 us: chain(): pl.pallas_call(functools.partial(chain_kernel, wide), out_shape=jax.Shape...]
    all_to_all x3 -> x0, blocking collectives: 114 us -> none  [the longest x1 56.5 us: body(): lax.all_to_all(tridiag_vectors, ('wide', 'narrow'), split_axis=1, concat_...]
    unnamed x6 -> x0, waiting for transfers between devices: 90.1 us -> none
    all_gather x4 -> x0, blocking collectives: 63.2 us -> none  [solve_chain(): lax.all_gather(remain, 'wide', axis=1, tiled=True)]
    psum x2 -> x0, blocking collectives: 52.3 us -> none  [body(): lax.psum(jnp.dot(current, reflectors[which], precision=HIGHEST), 'wide')]
    dot_general x13 -> x4, matrix products: 81.5 us -> 59.3 us  [the longest x2 36.1 us: body(): current = current - jnp.dot(coeffs, reflectors[which].T, precision=HIGHEST)]
    unnamed x19 -> x6, local copies, waits for them, and re-layouts: 14.2 us -> 8.28 us
  transfers between devices with their start and end apart: 3 -> 0, of which waited for: 3 -> 0; matrix products, arithmetic and copies ran while one was open for 0% -> 0% of each run, Pallas kernels for 0% -> 0%
where the time goes in v1:
time: 238 us; the launch traced here: 236 us
  Pallas kernels  159 us (67%)
  matrix products  59.3 us (25%)
  local copies, waits for them, and re-layouts  16.3 us (7%)
    pallas_call x1, Pallas kernels, chain(): pl.pallas_call(functools.partial(chain_kernel, wide), out_shape=jax.Shape...  67.5 us
    pallas_call x1, Pallas kernels, spread(): pl.pallas_call(functools.partial(spread_kernel, wide, narrow), out_shape=...  60.5 us
    dot_general x2, matrix products, body(): current = current - jnp.dot(coeffs, reflectors[which].T, precision=HIGHEST)  36.1 us
    pallas_call x2, Pallas kernels, coeffs_of(): pl.pallas_call(functools.partial(coeffs_kernel, wide), out_shape=jax.Shap...  31.5 us
    dot_general x2, matrix products, body(): products = jnp.dot(current, reflectors[which], precision=HIGHEST)  23.2 us
    unnamed x6, local copies, waits for them, and re-layouts  8.28 us

profile of v1, /device:TPU:0, one launch (start us, length us, event | category | flops | bytes accessed | tf_op | source)
XLA Modules:
  0.0 235.8 jit_solution(5087206050915460181)
XLA Ops:
  0.6 1.9 slice_bitcast_fusion
  2.5 60.5 %shard_map.68 = f32[16,4,16384]{2,1,0:T(4,128)} custom-call(f32[4,131072]{1,0:T(4,128)} %z_ref.1), custom_call_target="tpu_custom_call" | custom-call | tf_op jit(solution)/shard_map/pallas_call | solution.py:113
  63.0 3.1 %slice.20 = f32[8,4,16384]{2,1,0:T(4,128)} slice(f32[16,4,16384]{2,1,0:T(4,128)} %shard_map.68), slice={[0:8], [0:4], [0:16384]} | slice | bytes 4194304 | tf_op jit(solution)/shard_map/slice | solution.py:128
  66.0 2.0 reshape.10
  68.0 0.0 copy-start
  68.0 12.0 %fusion.4.x_ref = f32[32,256]{1,0:T(8,128)} fusion(f32[32,16384]{1,0:T(8,128)S(1)} %reshape.10, f32[2,16384,256]{2,1,0:T(8,128)} %param.6), kind=kOutput, calls=%fused_computation.6 | convolution fusion | flops 1610612736 | bytes 18907136 | tf_op jit(solution)/shard_map/dot_general | solution.py:317
  80.0 0.0 copy-done
  80.0 21.2 %shard_map.69 = f32[32,256]{1,0:T(8,128)} custom-call(f32[32,256]{1,0:T(8,128)} %fusion.4.x_ref, f32[256,256]{1,0:T(8,128)} %get-tuple-element.7.t_ref), custom_call_target="tpu_custom_call" | custom-call | tf_op jit(solution)/shard_map/pallas_call | solution.py:152
  101.2 18.6 %convolution_subtract_fusion.1 = f32[32,16384]{1,0:T(8,128)S(1)} fusion(f32[32,16384]{1,0:T(8,128)} %copy-done, f32[32,256]{1,0:T(8,128)} %shard_map.69, f32[2,16384,256]{2,1,0:T(8,128)} %param.6), kind=kOutput, calls=%fused_computation.1 | convolution fusion | flops 1611137024 | bytes 21004288 | tf_op jit(solution)/shard_map/dot_general | solution.py:319
  119.8 11.2 %fusion.1.x_ref = f32[32,256]{1,0:T(8,128)} fusion(f32[32,16384]{1,0:T(8,128)S(1)} %convolution_subtract_fusion.1, f32[2,16384,256]{2,1,0:T(8,128)} %param.6), kind=kOutput, calls=%fused_computation.3 | convolution fusion | flops 1610612736 | bytes 18907136 | tf_op jit(solution)/shard_map/dot_general | solution.py:317
  131.1 10.4 %shard_map.70 = f32[32,256]{1,0:T(8,128)} custom-call(f32[32,256]{1,0:T(8,128)} %fusion.1.x_ref, f32[256,256]{1,0:T(8,128)} %get-tuple-element.6.t_ref), custom_call_target="tpu_custom_call" | custom-call | tf_op jit(solution)/shard_map/pallas_call | solution.py:152
  141.4 17.4 %convolution_subtract_fusion = f32[32,16384]{1,0:T(8,128)S(1)} fusion(f32[32,16384]{1,0:T(8,128)S(1)} %convolution_subtract_fusion.1, f32[32,256]{1,0:T(8,128)} %shard_map.70, f32[2,16384,256]{2,1,0:T(8,128)} %param.6), kind=kOutput, calls=%fused_computation | convolution fusion | flops 1611137024 | bytes 21004288 | tf_op jit(solution)/shard_map/dot_general | solution.py:319
  158.9 0.0 copy-start.1
  158.9 1.3 copy-done.1
  160.2 0.1 slice.26
  160.3 0.5 reshape.11
  160.7 0.6 copy.13
  161.4 6.2 %copy.10.diag = f32[4,1536,192]{2,1,0:T(8,128)} copy(f32[4,1536,192]{1,2,0:T(8,128)} %param.9) | data formatting | bytes 9437184 | tf_op args[4]
  167.6 67.5 %shard_map.71 = f32[4,32,192]{2,1,0:T(8,128)S(1)} custom-call(f32[4,8,32,192]{3,2,1,0:T(8,128)S(1)} %bitcast.22, f32[6,192,1536]{2,1,0:T(8,128)} %lower.1, f32[4,1536,192]{2,1,0:T(8,128)} %copy.10.diag), custom_call_target="tpu_custom_call" | custom-call | tf_op jit(solution)/shard_map/pallas_call | solution.py:281
  235.1 0.7 copy.11
Async XLA Ops:
  68.0 12.0 %copy-start = (f32[32,16384]{1,0:T(8,128)}, f32[32,16384]{1,0:T(8,128)S(1)}, u32[]{:S(2)}) copy-start(f32[32,16384]{1,0:T(8,128)S(1)} %reshape.10) | copy-start | bytes 6291460
  158.9 1.3 copy-start.1

commit v2 on v1

--- a/solution.py
+++ b/solution.py
@@ -33,7 +33,10 @@
     )
 
 
-def spread_kernel(wide, narrow, z_ref, buf_ref, bounce, send1, recv1, send2, recv2, local_sem):
+def spread_kernel(
+    wide, narrow, z_ref, turned_ref, buf_ref, diag_ref, bounce, raw, turned,
+    send1, recv1, send2, recv2, local_sem, raw_sem, turned_sem,
+):
     w = lax.axis_index("wide")
     n = lax.axis_index("narrow")
     cols = buf_ref.shape[2]
@@ -47,12 +50,27 @@
     def slot(source):
         return (source * narrow + n) % wide
 
+    panels = turned_ref.shape[0]
+
+    def load(p):
+        return pltpu.make_async_copy(turned_ref.at[p], raw.at[p], raw_sem.at[p])
+
+    def store(p):
+        return pltpu.make_async_copy(turned.at[p], diag_ref.at[p], turned_sem.at[p])
+
+    def turn(p):
+        load(p).wait()
+        turned[p] = raw[p].T
+        store(p).start()
+
     greet((("wide", wide), ("narrow", narrow)))
     place = jnp.where(owner(w) == n, slot(w), wide + w)
     for k in range(1, wide):
         target = lax.rem(w + k, wide)
         remote(piece(target), buf_ref.at[place], send1.at[k], recv1.at[w], "wide", target).start()
 
+    for p in range(panels):
+        load(p).start()
     mine = owner(w) == n
 
     @pl.when(mine)
@@ -68,7 +86,9 @@
         remote(piece(w), buf_ref.at[s], send2.at[w], recv2.at[s], "narrow", owner(w)).start()
 
     for k in range(1, wide):
-        source = lax.rem(w + k, wide)
+        if k <= panels:
+            turn(k - 1)
+        source = lax.rem(w + wide - k, wide)
         to = owner(source)
         s = slot(source)
         here = jnp.where(to == n, s, wide + source)
@@ -80,9 +100,13 @@
                 buf_ref.at[wide + source], buf_ref.at[s], send2.at[source], recv2.at[s], "narrow", to
             ).start()
 
+    for p in range(wide - 1, panels):
+        turn(p)
     for k in range(1, wide):
         target = lax.rem(w + k, wide)
         remote(piece(target), buf_ref.at[place], send1.at[k], recv1.at[w], "wide", target).wait_send()
+    for p in range(panels):
+        store(p).wait()
     for source in range(wide):
         to = owner(source)
 
@@ -107,25 +131,34 @@
         pltpu.make_async_copy(bounce, buf_ref.at[slot(w)], local_sem.at[1]).wait()
 
 
-def spread(z, wide, narrow):
+def spread(z, turned, wide, narrow):
     rows, order = z.shape
     cols = order // wide
-    buf = pl.pallas_call(
+    panels, share, panel_rows = turned.shape
+    diag_shape = (panels, panel_rows, share)
+    buf, diag = pl.pallas_call(
         functools.partial(spread_kernel, wide, narrow),
-        out_shape=jax.ShapeDtypeStruct((2 * wide, rows, cols), jnp.float32),
-        in_specs=[pl.BlockSpec(memory_space=ANY)],
-        out_specs=pl.BlockSpec(memory_space=ANY),
+        out_shape=(
+            jax.ShapeDtypeStruct((2 * wide, rows, cols), jnp.float32),
+            jax.ShapeDtypeStruct(diag_shape, jnp.float32),
+        ),
+        in_specs=[pl.BlockSpec(memory_space=ANY)] * 2,
+        out_specs=[pl.BlockSpec(memory_space=ANY)] * 2,
         scratch_shapes=[
             VMEM((rows, cols), jnp.float32),
+            VMEM(turned.shape, jnp.float32),
+            VMEM(diag_shape, jnp.float32),
             pltpu.SemaphoreType.DMA((wide,)),
             pltpu.SemaphoreType.DMA((wide,)),
             pltpu.SemaphoreType.DMA((wide,)),
             pltpu.SemaphoreType.DMA((wide,)),
             pltpu.SemaphoreType.DMA((2,)),
+            pltpu.SemaphoreType.DMA((panels,)),
+            pltpu.SemaphoreType.DMA((panels,)),
         ],
         compiler_params=pltpu.CompilerParams(collective_id=0, has_side_effects=True),
-    )(z)
-    return buf[:wide].reshape(wide * rows, cols)
+    )(z, turned)
+    return buf[:wide].reshape(wide * rows, cols), diag
 
 
 def coeffs_kernel(wide, x_ref, t_ref, out_ref, slots, send, recv):
@@ -140,7 +173,7 @@
         remote(x_ref, slots.at[source], send.at[k], recv.at[source], "wide", source).wait_recv()
         total = total + slots[source]
     out_ref[...] = lax.dot_general(
-        total, t_ref[...], (((1,), (1,)), ((), ())),
+        t_ref[...], total, (((1,), (1,)), ((), ())),
         precision=HIGHEST, preferred_element_type=jnp.float32,
     )
     for k in range(1, wide):
@@ -151,7 +184,7 @@
 def coeffs_of(products, factor, wide, which):
     return pl.pallas_call(
         functools.partial(coeffs_kernel, wide),
-        out_shape=jax.ShapeDtypeStruct(products.shape, jnp.float32),
+        out_shape=jax.ShapeDtypeStruct((factor.shape[0], products.shape[0]), jnp.float32),
         in_specs=[pl.BlockSpec(memory_space=VMEM)] * 2,
         out_specs=pl.BlockSpec(memory_space=VMEM),
         scratch_shapes=[
@@ -161,6 +194,35 @@
         ],
         compiler_params=pltpu.CompilerParams(collective_id=1 + which, has_side_effects=True),
     )(products, factor)
+
+
+def update_kernel(z_ref, r_ref, c_ref, out_ref):
+    change = jnp.dot(
+        r_ref[0], c_ref[...], precision=HIGHEST, preferred_element_type=jnp.float32
+    )
+    out_ref[...] = z_ref[...] - change.T
+
+
+def update(current, reflectors, coeffs, which):
+    count, cols = current.shape
+    depth = reflectors.shape[2]
+    chunk = 1024 if cols % 1024 == 0 else 128
+    return pl.pallas_call(
+        update_kernel,
+        grid=(cols // chunk,),
+        out_shape=jax.ShapeDtypeStruct(current.shape, jnp.float32),
+        in_specs=[
+            pl.BlockSpec((count, chunk), lambda i: (0, i)),
+            pl.BlockSpec((1, chunk, depth), lambda i: (which, i, 0)),
+            pl.BlockSpec((depth, count), lambda i: (0, 0)),
+        ],
+        out_specs=pl.BlockSpec((count, chunk), lambda i: (0, i)),
+        cost_estimate=pl.CostEstimate(
+            flops=2 * count * cols * depth,
+            bytes_accessed=4 * cols * (depth + 2 * count),
+            transcendentals=0,
+        ),
+    )(current, reflectors, coeffs)
 
 
 def chain_kernel(
@@ -312,15 +374,17 @@
 def body(tridiag_vectors, reflectors, triangles, lower_blocks, diag_inverses):
     wide = lax.axis_size("wide")
     narrow = lax.axis_size("narrow")
-    current = spread(tridiag_vectors, wide, narrow)
+    current, diag = spread(
+        tridiag_vectors, diag_inverses.transpose(0, 2, 1), wide, narrow
+    )
     for which in (1, 0):
         products = jnp.dot(current, reflectors[which], precision=HIGHEST)
         coeffs = coeffs_of(products, triangles[which], wide, which)
-        current = current - jnp.dot(coeffs, reflectors[which].T, precision=HIGHEST)
+        current = update(current, reflectors, coeffs, which)
     panels, panel_rows, share = diag_inverses.shape
     tail = current[:, current.shape[1] - panels * panel_rows :]
     corner = tail.reshape(tail.shape[0], panels, wide, share).transpose(1, 2, 0, 3)
-    solved = chain(corner, lower_blocks, diag_inverses, wide)
+    solved = chain(corner, lower_blocks, diag, wide)
     return current, solved.transpose(1, 0, 2)
 
 

time: 238 us -> 238 us (level)
  Pallas kernels: 159 us -> 203 us
  matrix products: 59.3 us -> 24.6 us
  local copies, waits for them, and re-layouts: 16.3 us -> 8.93 us
    pallas_call x0 -> x2, Pallas kernels: none -> 41.7 us  [update(): pl.pallas_call(update_kernel, grid=(cols // chunk,), out_shape=jax.ShapeD...]
    dot_general x2 -> x0, matrix products: 36.1 us -> none  [body(): current = current - jnp.dot(coeffs, reflectors[which].T, precision=HIGHEST)]
    unnamed x6 -> x5, local copies, waits for them, and re-layouts: 8.28 us -> 0.75 us
    pallas_call x2, Pallas kernels: 31.5 us -> 35.8 us  [coeffs_of(): pl.pallas_call(functools.partial(coeffs_kernel, wide), out_shape=jax.Shap...]
    pallas_call x1, Pallas kernels: 60.5 us -> 57.4 us  [spread(): pl.pallas_call(functools.partial(spread_kernel, wide, narrow), out_shape=...]
where the time goes in v2:
time: 238 us; the launch traced here: 237 us
  Pallas kernels  203 us (85%)
  matrix products  24.6 us (10%)
  local copies, waits for them, and re-layouts  8.93 us (4%)
    pallas_call x1, Pallas kernels, chain(): pl.pallas_call(functools.partial(chain_kernel, wide), out_shape=jax.Shape...  67.8 us
    pallas_call x1, Pallas kernels, spread(): pl.pallas_call(functools.partial(spread_kernel, wide, narrow), out_shape=...  57.4 us
    pallas_call x2, Pallas kernels, update(): pl.pallas_call(update_kernel, grid=(cols // chunk,), out_shape=jax.ShapeD...  41.7 us
    pallas_call x2, Pallas kernels, coeffs_of(): pl.pallas_call(functools.partial(coeffs_kernel, wide), out_shape=jax.Shap...  35.8 us
    dot_general x2, matrix products, body(): products = jnp.dot(current, reflectors[which], precision=HIGHEST)  24.6 us

profile of v2, /device:TPU:0, one launch (start us, length us, event | category | flops | bytes accessed | tf_op | source)
XLA Modules:
  0.0 237.0 jit_solution(15723639068798329117)
XLA Ops:
  0.6 57.4 %shard_map.68 = (f32[16,4,16384]{2,1,0:T(4,128)}, f32[4,1536,192]{2,1,0:T(8,128)}) custom-call(f32[4,131072]{1,0:T(4,128)} %z_ref.1, f32[4,192,1536]{2,1,0:T(8,128)} %bitcast.19), custom_call_target="tpu_custom_call" | custom-call | tf_op jit(solution)/shard_map/pallas_call | solution.py:139
  58.0 3.1 %slice.18 = f32[8,4,16384]{2,1,0:T(4,128)} slice(f32[16,4,16384]{2,1,0:T(4,128)} %get-tuple-element.4), slice={[0:8], [0:4], [0:16384]} | slice | bytes 4194304 | tf_op jit(solution)/shard_map/slice | solution.py:161
  61.1 2.0 reshape.10.z_ref
  63.1 0.0 copy-start
  63.1 0.0 copy-start.1
  63.1 12.0 %fusion.2.x_ref = f32[32,256]{1,0:T(8,128)} fusion(f32[32,16384]{1,0:T(8,128)S(1)} %reshape.10.z_ref, f32[2,16384,256]{2,1,0:T(8,128)} %r_ref.3), kind=kOutput, calls=%fused_computation.2 | convolution fusion | flops 1610612736 | bytes 18907136 | tf_op jit(solution)/shard_map/dot_general | solution.py:381
  75.1 0.0 copy-done
  75.1 0.0 copy-done.1
  75.1 0.9 slice_bitcast_fusion
  76.0 24.4 %shard_map.69.c_ref = f32[256,32]{1,0:T(8,128)} custom-call(f32[32,256]{1,0:T(8,128)} %fusion.2.x_ref, f32[256,256]{1,0:T(8,128)} %get-tuple-element.11.t_ref), custom_call_target="tpu_custom_call" | custom-call | tf_op jit(solution)/shard_map/pallas_call | solution.py:185
  100.4 20.8 %shard_map.70.z_ref = f32[32,16384]{1,0:T(8,128)} custom-call(f32[32,16384]{1,0:T(8,128)} %copy-done, f32[2,16384,256]{2,1,0:T(8,128)} %r_ref.3, f32[256,32]{1,0:T(8,128)} %shard_map.69.c_ref), custom_call_target="tpu_custom_call" | custom-call | flops 268435456 | bytes 20971520 | tf_op jit(solution)/shard_map/pallas_call | solution.py:210
  121.3 12.6 %fusion.x_ref = f32[32,256]{1,0:T(8,128)} fusion(f32[32,16384]{1,0:T(8,128)} %shard_map.70.z_ref, f32[2,16384,256]{2,1,0:T(8,128)} %r_ref.3), kind=kOutput, calls=%fused_computation | convolution fusion | flops 1610612736 | bytes 18907136 | tf_op jit(solution)/shard_map/dot_general | solution.py:381
  133.9 11.4 %shard_map.71.c_ref = f32[256,32]{1,0:T(8,128)} custom-call(f32[32,256]{1,0:T(8,128)} %fusion.x_ref, f32[256,256]{1,0:T(8,128)} %get-tuple-element.10.t_ref), custom_call_target="tpu_custom_call" | custom-call | tf_op jit(solution)/shard_map/pallas_call | solution.py:185
  145.3 20.8 %shard_map.72 = f32[32,16384]{1,0:T(8,128)} custom-call(f32[32,16384]{1,0:T(8,128)} %shard_map.70.z_ref, f32[2,16384,256]{2,1,0:T(8,128)} %r_ref.3, f32[256,32]{1,0:T(8,128)} %shard_map.71.c_ref), custom_call_target="tpu_custom_call" | custom-call | flops 268435456 | bytes 20971520 | tf_op jit(solution)/shard_map/pallas_call | solution.py:210
  166.1 1.2 slice.24
  167.3 0.5 reshape.11
  167.8 0.6 copy.11
  168.4 67.8 %shard_map.73 = f32[4,32,192]{2,1,0:T(8,128)S(1)} custom-call(f32[4,8,32,192]{3,2,1,0:T(8,128)S(1)} %bitcast.17, f32[6,192,1536]{2,1,0:T(8,128)} %lower.1, f32[4,1536,192]{2,1,0:T(8,128)} %get-tuple-element.5.diag), custom_call_target="tpu_custom_call" | custom-call | tf_op jit(solution)/shard_map/pallas_call | solution.py:343
  236.2 0.7 copy.9
Async XLA Ops:
  63.1 12.0 %copy-start = (f32[32,16384]{1,0:T(8,128)}, f32[32,16384]{1,0:T(8,128)S(1)}, u32[]{:S(2)}) copy-start(f32[32,16384]{1,0:T(8,128)S(1)} %reshape.10.z_ref) | copy-start | bytes 6291460
  63.1 12.0 %copy-start.1 = (f32[2,256,256]{2,1,0:T(8,128)S(1)}, f32[2,256,256]{2,1,0:T(8,128)}, u32[]{:S(2)}) copy-start(f32[2,256,256]{2,1,0:T(8,128)} %param.7) | copy-start | bytes 1572868
